TPU v7x, 32 devices: a whole 2x2x4 slice. The times are simulated.
32 devices in a mesh: groups: 2 (over y), seq: 4 (over z), head: 4 (over x, core).
Axes of the slice: x: 2, y: 2, z: 4, core: 2. Of those that a mesh axis runs over, the one named last changes fastest.
Arguments:
- queries: bfloat16 [1536, 16, 576], P(('groups', 'seq'), 'head'), parts along dimension 0, may hold values from -40 to 40
- latent_kv: bfloat16 [1536, 576], P(('groups', 'seq')), parts along dimension 0, may hold values from -6 to 6
- adapter_ids: int32 [48], P(('groups', 'seq')), parts along dimension 0, may hold values from 0 to 4
- value_up: bfloat16 [16, 512, 128], P('head'), may hold values from -0.25 to 0.25
- output_weight: bfloat16 [2048, 2048], P('head'), may hold values from -0.1875 to 0.1875
- adapter_down: bfloat16 [2048, 80], P('head'), may hold values from -0.125 to 0.125
- adapter_up: bfloat16 [80, 2048], replicated, may hold values from -1.5 to 1.5
Outputs:
- mixed: bfloat16 [1536, 2048], P(('groups', 'seq'), 'head'), parts along dimension 0
There are 2 independent parts, one for each index of `groups`. A program takes and returns all parts, laid end to end along the dimension named above; an argument that names none is the same for every part. Nothing has to cross between parts.
All inputs are finite; a program needn't handle non-finite values.
Results may differ from a plain program's by a relative error of at most 0.017.
Values may be sent and summed in bfloat16 or wider, within the bound.
No kernel may reach another device: no remote copies, remote signals or barrier semaphores. Data moves between devices by JAX's collectives and lax.ppermute only.
A program may use at most 64 MiB of HBM per device.

v0:
```python
import math

import jax
import jax.numpy as jnp
from jax import lax
from jax.sharding import PartitionSpec as P

ROPE = 64
NOPE = 128
ADAPTERS = 5
RANK = 16
ADP_BLOCK = 32


def mirror_position(rows, tok_dev, count):
    shard = rows // tok_dev
    within = rows % tok_dev
    half = tok_dev // 2
    return jnp.where(
        within < half, shard * half + within, (2 * count - 1 - shard) * half + within - half
    )


def attend(totals, query_rows, row_position, carried, key_position, score_scale, latent_dim):
    row_max, row_sum, accumulated = totals
    scores = (
        lax.dot_general(
            query_rows, carried, (((1,), (1,)), ((), ())), preferred_element_type=jnp.float32
        )
        * score_scale
    )
    visible = key_position[None, :] <= row_position[:, None]
    scores = jnp.where(visible, scores, -1e30)
    new_max = jnp.maximum(row_max, jnp.max(scores, axis=1))
    weights = jnp.exp(scores - new_max[:, None])
    row_sum = jnp.sum(weights, axis=1)
    product = jnp.dot(
        weights.astype(jnp.bfloat16), carried[:, :latent_dim], preferred_element_type=jnp.float32
    )
    accumulated = product
    return (new_max, row_sum, accumulated)


def body(queries, latent_kv, adapter_ids, value_up, output_weight, adapter_down, adapter_up):
    seq_count = lax.axis_size("seq")
    own_index = lax.axis_index("seq")
    tok_rows = queries.shape[0]
    head_count = queries.shape[1]
    latent_width = latent_kv.shape[1]
    latent_dim = value_up.shape[1]
    score_scale = 1.0 / math.sqrt(NOPE + ROPE)
    query_rows = queries.reshape(tok_rows * head_count, latent_width)
    row_position = mirror_position(
        own_index * tok_rows + jnp.arange(tok_rows * head_count, dtype=jnp.int32) // head_count,
        tok_rows,
        seq_count,
    )
    start = (
        jnp.full((tok_rows * head_count,), -1e30, jnp.float32),
        jnp.zeros((tok_rows * head_count,), jnp.float32),
        jnp.zeros((tok_rows * head_count, latent_dim), jnp.float32),
    )
    carried = lax.all_gather(latent_kv, "seq", axis=0, tiled=True)
    key_position = mirror_position(
        jnp.arange(carried.shape[0], dtype=jnp.int32), tok_rows, seq_count
    )
    key_position = jnp.where(True, key_position, 2**30)
    totals = attend(start, query_rows, row_position, carried, key_position, score_scale, latent_dim)
    latent_out = (
        (totals[2] / totals[1][:, None])
        .astype(jnp.bfloat16)
        .reshape(tok_rows, head_count, latent_dim)
    )
    value_out = jnp.einsum("thl,hlv->thv", latent_out, value_up, preferred_element_type=jnp.float32)
    value_out = value_out.astype(jnp.bfloat16).reshape(tok_rows, head_count * value_up.shape[2])
    projected = jnp.dot(value_out, output_weight, preferred_element_type=jnp.float32)
    rank_part = jnp.dot(value_out, adapter_down, preferred_element_type=jnp.float32)
    owner = jnp.arange(ADAPTERS * RANK, dtype=jnp.int32) // RANK
    block_count = adapter_ids.shape[0]
    selector = (adapter_ids[:, None, None] == owner[None, None, :]).astype(jnp.float32)
    selector = jnp.broadcast_to(selector, (block_count, ADP_BLOCK, ADAPTERS * RANK)).reshape(
        tok_rows, ADAPTERS * RANK
    )
    mixed = lax.psum_scatter(
        projected.astype(jnp.bfloat16), "head", scatter_dimension=1, tiled=True
    ).astype(jnp.float32)
    rank_total = lax.psum(rank_part.astype(jnp.bfloat16), "head").astype(jnp.float32)
    columns = adapter_up.shape[1] // lax.axis_size("head")
    up_columns = lax.dynamic_slice_in_dim(adapter_up, lax.axis_index("head") * columns, columns, 1)
    mixed = mixed + jnp.dot(
        rank_total * selector, up_columns.astype(jnp.float32), precision=lax.Precision.HIGHEST
    )
    return mixed.astype(jnp.bfloat16)


def solution(mesh):
    return jax.shard_map(
        body,
        mesh=mesh,
        in_specs=(
            P(("groups", "seq"), "head", None),
            P(("groups", "seq"), None),
            P(("groups", "seq")),
            P("head", None, None),
            P("head", None),
            P("head", None),
            P(),
        ),
        out_specs=P(("groups", "seq"), "head"),
        check_vma=False,
    )
```

profile of v0, /device:TPU:0, one launch (start us, length us, event | category | flops | bytes accessed | tf_op | source)
XLA Modules:
  0.0 74.0 jit_solution(8393363527337615925)
XLA Ops:
  6.5 0.0 copy-start
  6.5 0.0 reduce-scatter.2.cloned.1.call-start
  6.6 23.8 %all_gather.3 = bf16[768,576]{1,0:T(8,128)(2,1)S(1)} all-gather(bf16[192,576]{1,0:T(8,128)(2,1)} %param.8), channel_id=1, replica_groups=mesh['groups'=2,'seq'=4,'head'=4] {'seq'}, dimensions={0}, use_global_device_ids=true | all-gather | bytes 1105920 | tf_op jit(solution)/shard_map/all_gather | solution.py:63
  30.4 2.4 %reshape.121 = bf16[768,576]{1,0:T(8,128)(2,1)} reshape(bf16[192,4,576]{2,1,0:T(4,128)(2,1)} %param.7) | data formatting | bytes 1769472 | tf_op jit(solution)/shard_map/reshape | solution.py:52
  32.8 2.3 %fusion.37 = (f32[768]{0:T(1024)S(1)}, f32[768,768]{0,1:T(8,128)S(1)}) fusion(bf16[768,576]{1,0:T(8,128)(2,1)} %reshape.121, bf16[768,576]{1,0:T(8,128)(2,1)S(1)} %all_gather.3, s32[768]{0:T(1024)S(1)} %get-tuple-element.8, s32[768]{0:T(1024)S(1)} %get-tuple-element.7), kind=kOutput, calls=%fused_computation.60 | convolution fusion | flops 681835776 | bytes 4137984 | tf_op jit(solution)/shard_map/dot_general | solution.py:27
  35.2 0.4 fusion
  35.6 1.7 %divide_convert_fusion = bf16[768,512]{1,0:T(8,128)(2,1)} fusion(f32[768,768]{0,1:T(8,128)S(1)} %get-tuple-element.6, f32[768]{0:T(1024)S(1)} %broadcast_maximum_fusion, bf16[768,576]{1,0:T(8,128)(2,1)S(1)} %all_gather.3, f32[768]{0:T(1024)S(1)} %fusion), kind=kOutput, calls=%fused_computation.5 | convolution fusion | flops 605945856 | bytes 3940352 | tf_op jit(solution)/shard_map/dot_general | solution.py:37
  37.3 1.7 %reshape.122 = bf16[192,4,512]{2,1,0:T(4,128)(2,1)S(1)} reshape(bf16[768,512]{1,0:T(8,128)(2,1)} %divide_convert_fusion) | data formatting | bytes 1572864 | tf_op jit(solution)/shard_map/reshape | solution.py:72
  39.0 1.4 %fusion.5 = bf16[4,24,8,128]{3,2,1,0:T(8,128)(2,1)S(1)} fusion(bf16[4,512,128]{2,1,0:T(8,128)(2,1)} %param.10, bf16[192,4,512]{2,1,0:T(4,128)(2,1)S(1)} %reshape.122), kind=kOutput, calls=%fused_computation.10 | convolution fusion | flops 100761600 | bytes 1507328 | tf_op jit(solution)/shard_map/thl,hlv->thv/dot_general | solution.py:74
  40.4 0.0 copy-done
  40.4 0.0 copy-start.2
  40.4 0.0 copy-start.1
  40.4 1.5 %convolution_convert_fusion = bf16[192,2048]{1,0:T(8,128)(2,1)} fusion(bf16[512,2048]{1,0:T(8,128)(2,1)S(1)} %copy-done, bf16[4,24,8,128]{3,2,1,0:T(8,128)(2,1)S(1)} %fusion.5), kind=kOutput, calls=%fused_computation | convolution fusion | flops 403046400 | bytes 3080192 | tf_op jit(solution)/shard_map/dot_general | solution.py:76
  41.9 0.0 reduce-scatter.2.cloned.1.call-update
  41.9 0.0 copy-done.2
  41.9 0.2 convolution_convert_fusion.2
  42.1 10.5 %psum.7 = bf16[192,80]{1,0:T(8,128)(2,1)S(1)} all-reduce(bf16[192,80]{1,0:T(8,128)(2,1)S(1)} %convolution_convert_fusion.2), channel_id=1, replica_groups=mesh['groups'=2,'seq'=4,'head'=4] {'head'}, use_global_device_ids=true, to_apply=%region_3.4 | all-reduce | flops 15360 | bytes 61440 | tf_op jit(solution)/shard_map/psum | solution.py:87
  52.7 0.0 copy-done.1
  52.7 0.1 compare_convert_fusion
  52.8 12.4 %reduce-scatter.2.cloned.1.call-done = bf16[192,512]{1,0:T(8,128)(2,1)} async-done(((bf16[192,2048]{1,0:T(8,128)(2,1)}), bf16[192,512]{1,0:T(8,128)(2,1)}) %reduce-scatter.2.cloned.1.call-update) | async-done | bytes 196624 | tf_op jit(solution)/shard_map/reduce_scatter | solution.py:84
  65.2 2.0 %fusion.4 = bf16[192,512]{1,0:T(8,128)(2,1)} fusion(f32[192,80]{1,0:T(8,128)S(1)} %bitcast_multiply_fusion, bf16[192,512]{1,0:T(8,128)(2,1)} %reduce-scatter.2.cloned.1.call-done, bf16[80,2048]{1,0:T(8,128)(2,1)} %param.13, s32[]{:T(128)S(6)} %select_n.85), kind=kOutput, calls=%fused_computation.8 | convolution fusion | flops 94666752 | bytes 536580 | tf_op jit(solution)/shard_map/dot_general | solution.py:90
  (4 shorter events, 0.0 us)
Async XLA Ops:
  6.5 33.9 %copy-start = (bf16[512,2048]{1,0:T(8,128)(2,1)S(1)}, bf16[512,2048]{1,0:T(8,128)(2,1)}, u32[]{:S(2)}) copy-start(bf16[512,2048]{1,0:T(8,128)(2,1)} %param.11) | copy-start | bytes 6291460
  6.5 58.7 %reduce-scatter.2.cloned.1.call-start = ((), (), s32[]{:S(2)}) async-start(), calls=%async_computation.1 | async-start | bytes 983040 | tf_op jit(solution)/shard_map/reduce_scatter | solution.py:84
  40.4 1.5 %copy-start.2 = (bf16[512,80]{0,1:T(8,128)(2,1)S(1)}, bf16[512,80]{0,1:T(8,128)(2,1)}, u32[]{:S(2)}) copy-start(bf16[512,80]{0,1:T(8,128)(2,1)} %param.12) | copy-start | bytes 245764
  40.4 12.3 %copy-start.1 = (s32[6]{0:T(128)S(1)}, s32[6]{0:T(128)}, u32[]{:S(2)}) copy-start(s32[6]{0:T(128)} %param.9) | copy-start | bytes 76
Sparse Core Ops, SparseCore 0:
  42.1 23.1 reduce-scatter.1
where the time goes:
time: 74.3 us; the launch traced here: 74 us
  blocking collectives  34.3 us (46%)
  between operations  13.5 us (18%)
  waiting for transfers between devices  12.4 us (17%)
  matrix products  9.12 us (12%)
  local copies, waits for them, and re-layouts  4.14 us (6%)
    all_gather x1, blocking collectives, body(): carried = lax.all_gather(latent_kv, 'seq', axis=0, tiled=True)  23.8 us
    reduce_scatter x1, waiting for transfers between devices, body(): lax.psum_scatter(projected.astype(jnp.bfloat16), 'head', scatter_dimensio...  12.4 us
    psum x1, blocking collectives, body(): lax.psum(rank_part.astype(jnp.bfloat16), 'head').astype(jnp.float32)  10.5 us
    reshape x1, local copies, waits for them, and re-layouts, body(): query_rows = queries.reshape(tok_rows * head_count, latent_width)  2.44 us
    dot_general x1, matrix products, attend(): lax.dot_general(query_rows, carried, (((1,), (1,)), ((), ())), preferred_...  2.34 us
    dot_general x1, matrix products, body(): jnp.dot(rank_total * selector, up_columns.astype(jnp.float32), precision=...  1.96 us
    dot_general x1, matrix products, attend(): jnp.dot(weights.astype(jnp.bfloat16), carried[:, :latent_dim], preferred_...  1.71 us
    reshape x1, local copies, waits for them, and re-layouts, body(): latent_out = (totals[2] / totals[1][:, None]).astype(jnp.bfloat16).reshap...  1.68 us
  transfers between devices with their start and end apart: 1, of which 1 were waited for; matrix products, arithmetic and copies ran while one was open for 0% of the time, Pallas kernels for 0%

commit v1 on v0

v1 whole, which is shorter than its diff:
```python
import math

import jax
import jax.numpy as jnp
from jax import lax
from jax.sharding import PartitionSpec as P

ROPE = 64
NOPE = 128
ADAPTERS = 5
RANK = 16
ADP_BLOCK = 32


def block_start(shard, second, half, count):
    return jnp.where(second, (2 * count - 1 - shard) * half, shard * half)


def gather_latents(latent_kv):
    count = lax.axis_size("seq")
    heads = lax.axis_size("head")
    me = lax.axis_index("seq")
    core = lax.axis_index("head") % 2
    half = latent_kv.shape[0] // 2
    steps = jnp.arange(half, dtype=jnp.int32)
    own_half = lax.dynamic_slice_in_dim(latent_kv, core * half, half, 0)
    keys = [latent_kv]
    positions = [block_start(me, False, half, count) + steps, block_start(me, True, half, count) + steps]
    arrived = []
    for shift in range(1, count):
        pairs = []
        for source in range(count):
            target = (source - shift) % count
            for head in range(heads):
                if head % 2 == 0 or target < source:
                    pairs.append((source * heads + head, target * heads + head))
        arrived.append(lax.ppermute(own_half, ("seq", "head"), pairs))
        shard = (me + shift) % count
        positions.append(block_start(shard, core == 1, half, count) + steps)
    mine = jnp.concatenate(arrived, axis=0)
    other = lax.ppermute(mine, "head", [(head, head ^ 1) for head in range(heads)])
    for shift in range(1, count):
        shard = (me + shift) % count
        positions.append(block_start(shard, core == 0, half, count) + steps)
    return jnp.concatenate([latent_kv, mine, other], axis=0), jnp.concatenate(positions)


def body(queries, latent_kv, adapter_ids, value_up, output_weight, adapter_down, adapter_up):
    seq_count = lax.axis_size("seq")
    heads = lax.axis_size("head")
    own_index = lax.axis_index("seq")
    head_index = lax.axis_index("head")
    tok_rows, head_count, latent_width = queries.shape
    latent_dim = value_up.shape[1]
    half = tok_rows // 2
    score_scale = 1.0 / math.sqrt(NOPE + ROPE)
    query_rows = queries.transpose(1, 0, 2)
    steps = jnp.arange(half, dtype=jnp.int32)
    row_position = jnp.concatenate(
        [
            block_start(own_index, False, half, seq_count) + steps,
            block_start(own_index, True, half, seq_count) + steps,
        ]
    )
    carried, key_position = gather_latents(latent_kv)
    scores = (
        jnp.einsum("htl,ul->htu", query_rows, carried, preferred_element_type=jnp.float32)
        * score_scale
    )
    visible = key_position[None, :] <= row_position[:, None]
    scores = jnp.where(visible[None], scores, -1e30)
    row_max = jnp.max(scores, axis=2, keepdims=True)
    weights = jnp.exp(scores - row_max)
    row_sum = jnp.sum(weights, axis=2, keepdims=True)
    product = jnp.einsum(
        "htu,ul->htl",
        weights.astype(jnp.bfloat16),
        carried[:, :latent_dim],
        preferred_element_type=jnp.float32,
    )
    latent_out = (product / row_sum).astype(jnp.bfloat16)
    value_out = jnp.einsum("htl,hlv->thv", latent_out, value_up, preferred_element_type=jnp.float32)
    value_out = value_out.astype(jnp.bfloat16).reshape(tok_rows, head_count * value_up.shape[2])
    rank_part = jnp.dot(value_out, adapter_down, preferred_element_type=jnp.float32)
    owner = jnp.arange(ADAPTERS * RANK, dtype=jnp.int32) // RANK
    block_count = adapter_ids.shape[0]
    chosen = adapter_ids[:, None, None] == owner[None, None, :]
    chosen = jnp.broadcast_to(chosen, (block_count, ADP_BLOCK, ADAPTERS * RANK)).reshape(
        tok_rows, ADAPTERS * RANK
    )
    selected = jnp.where(chosen, rank_part, 0.0)
    high = selected.astype(jnp.bfloat16)
    low = (selected - high.astype(jnp.float32)).astype(jnp.bfloat16)
    left = jnp.concatenate([value_out, high, low], axis=1)
    right = jnp.concatenate([output_weight, adapter_up, adapter_up], axis=0)
    columns = adapter_up.shape[1] // heads
    pair, core = head_index // 2, head_index % 2
    pairs = heads // 2

    def share(owner_head):
        part = lax.dynamic_slice_in_dim(right, owner_head * columns, columns, 1)
        return jnp.dot(left, part, preferred_element_type=jnp.float32)

    order = [(pair + shift) % pairs for shift in range(pairs)]
    sent = jnp.concatenate([share(p * 2 + 1 - core).astype(jnp.bfloat16) for p in order], axis=1)
    received = lax.ppermute(sent, "head", [(head, head ^ 1) for head in range(heads)])
    kept = [
        share(p * 2 + core)
        + received[:, i * columns : (i + 1) * columns].astype(jnp.float32)
        for i, p in enumerate(order)
    ]
    mixed = kept[0]
    for shift in range(1, pairs):
        moves = [(head, (head + 2 * shift) % heads) for head in range(heads)]
        mixed += lax.ppermute(kept[shift].astype(jnp.bfloat16), "head", moves).astype(jnp.float32)
    return mixed.astype(jnp.bfloat16)


def solution(mesh):
    return jax.shard_map(
        body,
        mesh=mesh,
        in_specs=(
            P(("groups", "seq"), "head", None),
            P(("groups", "seq"), None),
            P(("groups", "seq")),
            P("head", None, None),
            P("head", None),
            P("head", None),
            P(),
        ),
        out_specs=P(("groups", "seq"), "head"),
        check_vma=False,
    )
```

time: 74.3 us -> 46.1 us (0.62)
  blocking collectives: 34.3 us -> 0 us
  starting transfers between devices: 0.01 us -> 15 us
  between operations: 13.5 us -> 0.26 us
  waiting for transfers between devices: 12.4 us -> 7.03 us
  local copies, waits for them, and re-layouts: 4.14 us -> 8.76 us
  matrix products: 9.12 us -> 12.5 us
  other arithmetic: 0.48 us -> 2.07 us
    all_gather x1 -> x0, blocking collectives: 23.8 us -> none  [body(): carried = lax.all_gather(latent_kv, 'seq', axis=0, tiled=True)]
    ppermute x0 -> x6, starting transfers between devices: none -> 15 us  [the longest x3 12.7 us: gather_latents(): arrived.append(lax.ppermute(own_half, ('seq', 'head'), pairs))]
    reduce_scatter x1 -> x0, waiting for transfers between devices: 12.4 us -> none  [body(): lax.psum_scatter(projected.astype(jnp.bfloat16), 'head', scatter_dimensio...]
    psum x1 -> x0, blocking collectives: 10.5 us -> none  [body(): lax.psum(rank_part.astype(jnp.bfloat16), 'head').astype(jnp.float32)]
    ppermute x0 -> x6, waiting for transfers between devices: none -> 7.03 us  [the longest x1 3.79 us: body(): lax.ppermute(kept[shift].astype(jnp.bfloat16), 'head', moves)]
    unnamed x6 -> x9, local copies, waits for them, and re-layouts: 0.02 us -> 5.12 us
    reshape x2, local copies, waits for them, and re-layouts: 4.12 us -> 1.06 us  [the longest x1 0.96 us: body(): value_out.astype(jnp.bfloat16)]
    dot_general x5 -> x6, matrix products: 8.92 us -> 11.3 us  [the longest x4 5.7 us: share(): return jnp.dot(left, part, preferred_element_type=jnp.float32)]
  transfers between devices with their start and end apart: 1 -> 6, of which waited for: 1 -> 4; matrix products, arithmetic and copies ran while one was open for 0% -> 14% of each run, Pallas kernels for 0% -> 0%
where the time goes in v1:
time: 46.1 us; the launch traced here: 45.6 us
  starting transfers between devices  15 us (33%)
  matrix products  12.5 us (27%)
  local copies, waits for them, and re-layouts  8.76 us (19%)
  waiting for transfers between devices  7.03 us (15%)
  other arithmetic  2.07 us (4%)
    ppermute x3, starting transfers between devices, gather_latents(): arrived.append(lax.ppermute(own_half, ('seq', 'head'), pairs))  12.7 us
    dot_general x4, matrix products, share(): return jnp.dot(left, part, preferred_element_type=jnp.float32)  5.7 us
    unnamed x9, local copies, waits for them, and re-layouts  5.12 us
    ppermute x1, waiting for transfers between devices, body(): lax.ppermute(kept[shift].astype(jnp.bfloat16), 'head', moves)  3.79 us
    dot_general x1, matrix products, body(): jnp.einsum('htl,hlv->thv', latent_out, value_up, preferred_element_type=j...  3.1 us
    dot_general x1, matrix products, body(): jnp.einsum('htl,ul->htu', query_rows, carried, preferred_element_type=jnp...  2.52 us
    ppermute x1, starting transfers between devices, body(): lax.ppermute(kept[shift].astype(jnp.bfloat16), 'head', moves)  1.97 us
    ppermute x1, waiting for transfers between devices, body(): lax.ppermute(sent, 'head', [(head, head ^ 1) for head in range(heads)])  1.59 us
  transfers between devices with their start and end apart: 6, of which 4 were waited for; matrix products, arithmetic and copies ran while one was open for 14% of the time, Pallas kernels for 0%

profile of v1, /device:TPU:0, one launch (start us, length us, event | category | flops | bytes accessed | tf_op | source)
XLA Modules:
  0.0 45.6 jit_solution(6368411852100890356)
XLA Ops:
  0.0 0.0 copy-start
  0.0 1.2 %copy.14 = bf16[192,576]{0,1:T(8,128)(2,1)S(1)} copy(bf16[192,576]{1,0:T(8,128)(2,1)} %param.8) | data formatting | bytes 442368 | tf_op args[1]
  1.2 0.0 copy-start.1
  1.2 0.1 constant_dynamic-slice_fusion
  1.3 5.0 %collective-permute-start.2 = (bf16[96,576]{0,1:T(8,128)(2,1)S(1)}, bf16[96,576]{0,1:T(8,128)(2,1)S(1)}, u32[]{:S(2)}, u32[]{:S(2)}) collective-permute-start(bf16[96,576]{0,1:T(8,128)(2,1)S(1)} %constant_dynamic-slice_fusion), channel_id=1, source_target_pairs={{0,4},{2,6},{4,8},{6,10},{8,12},{10,14},{12,0},{13,1},{14,2},{15,3... | collective-permute-start | bytes 331784 | tf_op jit(solution)/shard_map/ppermute | solution.py:37
  6.3 4.5 %collective-permute-start.1 = (bf16[96,576]{0,1:T(8,128)(2,1)S(1)}, bf16[96,576]{0,1:T(8,128)(2,1)S(1)}, u32[]{:S(2)}, u32[]{:S(2)}) collective-permute-start(bf16[96,576]{0,1:T(8,128)(2,1)S(1)} %constant_dynamic-slice_fusion), channel_id=1, source_target_pairs={{0,8},{2,10},{4,12},{6,14},{8,0},{9,1},{10,2},{11,3},{12,4},{13,5}... | collective-permute-start | bytes 331784 | tf_op jit(solution)/shard_map/ppermute | solution.py:37
  10.8 3.3 %collective-permute-start = (bf16[96,576]{0,1:T(8,128)(2,1)S(1)}, bf16[96,576]{0,1:T(8,128)(2,1)S(1)}, u32[]{:S(2)}, u32[]{:S(2)}) collective-permute-start(bf16[96,576]{0,1:T(8,128)(2,1)S(1)} %constant_dynamic-slice_fusion), channel_id=1, source_target_pairs={{0,12},{2,14},{4,0},{5,1},{6,2},{7,3},{8,4},{9,5},{10,6},{11,7},{1... | collective-permute-start | bytes 331784 | tf_op jit(solution)/shard_map/ppermute | solution.py:37
  14.1 0.0 copy-start.2
  14.1 3.2 %constant_dynamic-update-slice_fusion.2 = bf16[672,2048]{1,0:T(8,128)(2,1)} fusion(bf16[512,2048]{1,0:T(8,128)(2,1)} %param.11), kind=kLoop, calls=%fused_computation.37 | loop fusion | bytes 4194304
  17.4 0.1 pad_add_fusion
  17.4 0.1 concatenate.22
  17.5 0.2 broadcast_compare_fusion
  17.7 0.0 copy-done.1
  17.7 0.7 %constant_dynamic-update-slice_fusion.1 = bf16[672,2048]{1,0:T(8,128)(2,1)} fusion(bf16[672,2048]{1,0:T(8,128)(2,1)} %constant_dynamic-update-slice_fusion.2, bf16[80,2048]{1,0:T(8,128)(2,1)S(1)} %copy-done.1), kind=kLoop, calls=%fused_computation.36 | loop fusion | bytes 655360
  18.4 0.0 collective-permute-done.2
  18.4 0.0 collective-permute-done.1
  18.4 0.8 %collective-permute-done = bf16[96,576]{0,1:T(8,128)(2,1)S(1)} collective-permute-done((bf16[96,576]{0,1:T(8,128)(2,1)S(1)}, bf16[96,576]{0,1:T(8,128)(2,1)S(1)}, u32[]{:S(2)}, u32[]{:S(2)}) %collective-permute-start) | collective-permute-done | bytes 110624 | tf_op jit(solution)/shard_map/ppermute | solution.py:37
  19.3 0.2 pad_maximum_fusion
  19.5 0.1 collective-permute-start.3
  19.6 0.0 copy-done.2
  19.6 0.1 broadcast_compare_fusion.1
  19.7 0.1 copy.17
  19.8 0.8 %constant_dynamic-update-slice_fusion = bf16[672,2048]{1,0:T(8,128)(2,1)} fusion(bf16[672,2048]{1,0:T(8,128)(2,1)} %constant_dynamic-update-slice_fusion.1, bf16[80,2048]{1,0:T(8,128)(2,1)S(1)} %copy-done.1), kind=kLoop, calls=%fused_computation.35 | loop fusion | bytes 655360 | tf_op jit(solution)/shard_map/concatenate | solution.py:95
  20.6 0.8 %collective-permute-done.3 = bf16[288,576]{0,1:T(8,128)(2,1)S(1)} collective-permute-done((bf16[288,576]{0,1:T(8,128)(2,1)S(1)}, bf16[288,576]{0,1:T(8,128)(2,1)S(1)}, u32[]{:S(2)}, u32[]{:S(2)}) %collective-permute-start.3) | collective-permute-done | bytes 331808 | tf_op jit(solution)/shard_map/ppermute | solution.py:41
  21.4 1.4 %concatenate.25 = bf16[768,576]{0,1:T(8,128)(2,1)} concatenate(bf16[192,576]{0,1:T(8,128)(2,1)S(1)} %copy.14, bf16[96,576]{0,1:T(8,128)(2,1)S(1)} %collective-permute-done, bf16[96,576]{0,1:T(8,128)(2,1)S(1)} %collective-permute-done.1, bf16[96,576]{0,1:T(8,128)(2,1)S(1)} %collective-permute-done.2, bf16[288,576]{0,1:T(8,128)(2,1)S(1)} %collective-permute-done.3), dimensions={0} | concatenate | bytes 1769472 | tf_op jit(solution)/shard_map/concatenate | solution.py:45
  22.8 0.0 copy-done
  22.8 2.5 %fusion.2 = (f32[4,192]{1,0:T(4,128)S(1)}, f32[768,4,192]{0,2,1:T(8,128)S(1)}) fusion(pred[192,768]{1,0:T(8,128)(4,1)S(1)} %broadcast_compare_fusion, bf16[4,192,576]{2,0,1:T(4,128)(2,1)S(1)} %bitcast.36, bf16[768,576]{0,1:T(8,128)(2,1)} %concatenate.25), kind=kOutput, calls=%fused_computation.4 | convolution fusion | flops 681245952 | bytes 4279296 | tf_op jit(solution)/shard_map/htl,ul->htu/dot_general | solution.py:67
  25.3 0.7 %fusion = f32[4,192]{1,0:T(4,128)S(1)} fusion(f32[768,4,192]{0,2,1:T(8,128)S(1)} %get-tuple-element.8, f32[4,192]{1,0:T(4,128)S(1)} %get-tuple-element.7, pred[192,768]{1,0:T(8,128)(4,1)S(1)} %broadcast_compare_fusion), kind=kLoop, calls=%fused_computation.2 | loop fusion | flops 2358528 | bytes 2512896 | tf_op jit(solution)/shard_map/reduce_sum | solution.py:74
  26.0 3.1 %fusion.17 = bf16[4,24,8,128]{3,2,1,0:T(8,128)(2,1)} fusion(bf16[4,512,128]{2,1,0:T(8,128)(2,1)} %param.10, f32[768,4,192]{0,2,1:T(8,128)S(1)} %get-tuple-element.8, f32[4,192]{1,0:T(4,128)S(1)} %get-tuple-element.7, pred[192,768]{1,0:T(8,128)(4,1)S(1)} %broadcast_compare_fusion, bf16[768,576]{0,1:T(8,128)(2,1)} %concatenate.25, f32[4,192]{1,0:T(4,128)S(1)} %fusion), kind=kOutput, calls=%fused_computation.14 | convolution fusion | flops 707887104 | bytes 4020224 | tf_op jit(solution)/shard_map/htl,hlv->thv/dot_general | solution.py:82
  29.1 1.0 %copy.29 = bf16[4,24,8,128]{3,2,0,1:T(8,128)(2,1)S(1)} copy(bf16[4,24,8,128]{3,2,1,0:T(8,128)(2,1)} %fusion.17) | data formatting | bytes 393216 | tf_op jit(solution)/shard_map/reshape | solution.py:83
  30.1 1.2 %subtract_convert_fusion = (bf16[192,80]{0,1:T(8,128)(2,1)S(1)}, bf16[192,80]{0,1:T(8,128)(2,1)S(1)}) fusion(pred[192,80]{0,1:T(8,128)(4,1)S(1)} %copy.17, bf16[512,80]{0,1:T(8,128)(2,1)} %param.12, bf16[4,24,8,128]{3,2,1,0:T(8,128)(2,1)} %fusion.17), kind=kOutput, calls=%fused_computation.34 | convolution fusion | flops 15805440 | bytes 355328 | tf_op jit(solution)/shard_map/dot_general | solution.py:84
  31.3 0.1 copy.19
  31.4 0.1 copy.18
  31.5 1.4 %convolution_convert_fusion = bf16[192,512]{1,0:T(8,128)(2,1)S(1)} fusion(bf16[672,2048]{1,0:T(8,128)(2,1)} %constant_dynamic-update-slice_fusion, s32[]{:T(128)S(6)} %select_n.113, bf16[192,80]{1,0:T(8,128)(2,1)S(1)} %copy.19, bf16[192,80]{1,0:T(8,128)(2,1)S(1)} %copy.18, bf16[192,512]{1,0:T(8,128)(2,1)S(1)} %bitcast.37), kind=kOutput, calls=%fused_computation.12 | convolution fusion | flops 132993024 | bytes 1142788 | tf_op jit(solution)/shard_map/dot_general | solution.py:102
  32.9 1.4 %convolution_convert_fusion.1 = bf16[192,512]{1,0:T(8,128)(2,1)S(1)} fusion(bf16[672,2048]{1,0:T(8,128)(2,1)} %constant_dynamic-update-slice_fusion, s32[]{:T(128)S(6)} %select_n.111, bf16[192,80]{1,0:T(8,128)(2,1)S(1)} %copy.19, bf16[192,80]{1,0:T(8,128)(2,1)S(1)} %copy.18, bf16[192,512]{1,0:T(8,128)(2,1)S(1)} %bitcast.38), kind=kOutput, calls=%fused_computation.13 | convolution fusion | flops 132993024 | bytes 1142788 | tf_op jit(solution)/shard_map/dot_general | solution.py:102
  34.4 0.2 collective-permute-start.4
  34.6 1.6 %collective-permute-done.4 = bf16[192,1024]{1,0:T(8,128)(2,1)S(1)} collective-permute-done((bf16[192,1024]{1,0:T(8,128)(2,1)S(1)}, bf16[192,1024]{1,0:T(8,128)(2,1)S(1)}, u32[]{:S(2)}, u32[]{:S(2)}) %collective-permute-start.4) | collective-permute-done | bytes 393248 | tf_op jit(solution)/shard_map/ppermute | solution.py:106
  36.2 1.4 %add_convert_fusion.1 = bf16[192,512]{1,0:T(8,128)(2,1)S(1)} fusion(bf16[192,1024]{1,0:T(8,128)(2,1)S(1)} %collective-permute-done.4, bf16[672,2048]{1,0:T(8,128)(2,1)} %constant_dynamic-update-slice_fusion, s32[]{:T(128)S(6)} %select_n.114, bf16[192,80]{1,0:T(8,128)(2,1)S(1)} %copy.19, bf16[192,80]{1,0:T(8,128)(2,1)S(1)} %copy.18, ...), kind=kOutput, calls=%fused_computation.30 | convolution fusion | flops 133189632 | bytes 1339396 | tf_op jit(solution)/shard_map/dot_general | solution.py:102
  37.6 2.0 %collective-permute-start.5 = (bf16[192,512]{1,0:T(8,128)(2,1)S(1)}, bf16[192,512]{1,0:T(8,128)(2,1)S(1)}, u32[]{:S(2)}, u32[]{:S(2)}) collective-permute-start(bf16[192,512]{1,0:T(8,128)(2,1)S(1)} %add_convert_fusion.1), channel_id=1, source_target_pairs={{0,2},{1,3},{2,0},{3,1},{4,6},{5,7},{6,4},{7,5},{8,10},{9,11},{10,... | collective-permute-start | bytes 589832 | tf_op jit(solution)/shard_map/ppermute | solution.py:115
  39.6 1.4 %fusion.28 = f32[192,512]{1,0:T(8,128)S(1)} fusion(bf16[672,2048]{1,0:T(8,128)(2,1)} %constant_dynamic-update-slice_fusion, s32[]{:T(128)S(6)} %select_n.110, bf16[192,80]{1,0:T(8,128)(2,1)S(1)} %copy.19, bf16[192,80]{1,0:T(8,128)(2,1)S(1)} %copy.18, bf16[192,512]{1,0:T(8,128)(2,1)S(1)} %bitcast.40), kind=kOutput, calls=%fused_computation.25 | convolution fusion | flops 132894720 | bytes 1339396 | tf_op jit(solution)/shard_map/dot_general | solution.py:102
  41.0 3.8 %collective-permute-done.5 = bf16[192,512]{1,0:T(8,128)(2,1)S(1)} collective-permute-done((bf16[192,512]{1,0:T(8,128)(2,1)S(1)}, bf16[192,512]{1,0:T(8,128)(2,1)S(1)}, u32[]{:S(2)}, u32[]{:S(2)}) %collective-permute-start.5) | collective-permute-done | bytes 196640 | tf_op jit(solution)/shard_map/ppermute | solution.py:115
  44.8 0.8 %add_convert_fusion = bf16[192,512]{1,0:T(8,128)(2,1)} fusion(bf16[192,512]{1,0:T(8,128)(2,1)S(1)} %collective-permute-done.5, f32[192,512]{1,0:T(8,128)S(1)} %fusion.28, bf16[192,1024]{1,0:T(8,128)(2,1)S(1)} %collective-permute-done.4), kind=kLoop, calls=%fused_computation.29 | loop fusion | flops 491520 | bytes 983040 | tf_op jit(solution)/shard_map/convert_element_type | solution.py:116
  (7 shorter events, 0.1 us)
Async XLA Ops:
  0.0 22.8 %copy-start = (bf16[192,4,576]{2,1,0:T(4,128)(2,1)S(1)}, bf16[192,4,576]{2,1,0:T(4,128)(2,1)}, u32[]{:S(2)}) copy-start(bf16[192,4,576]{2,1,0:T(4,128)(2,1)} %param.7) | copy-start | bytes 2654212
  1.2 16.5 %copy-start.1 = (bf16[80,2048]{1,0:T(8,128)(2,1)S(1)}, bf16[80,2048]{1,0:T(8,128)(2,1)}, u32[]{:S(2)}) copy-start(bf16[80,2048]{1,0:T(8,128)(2,1)} %param.13) | copy-start | bytes 983044
  1.3 17.1 %collective-permute-start.2 = (bf16[96,576]{0,1:T(8,128)(2,1)S(1)}, bf16[96,576]{0,1:T(8,128)(2,1)S(1)}, u32[]{:S(2)}, u32[]{:S(2)}) collective-permute-start(bf16[96,576]{0,1:T(8,128)(2,1)S(1)} %constant_dynamic-slice_fusion), channel_id=1, source_target_pairs={{0,4},{2,6},{4,8},{6,10},{8,12},{10,14},{12,0},{13,1},{14,2},{15,3... | collective-permute-start | bytes 331784 | tf_op jit(solution)/shard_map/ppermute | solution.py:37
  6.3 12.1 %collective-permute-start.1 = (bf16[96,576]{0,1:T(8,128)(2,1)S(1)}, bf16[96,576]{0,1:T(8,128)(2,1)S(1)}, u32[]{:S(2)}, u32[]{:S(2)}) collective-permute-start(bf16[96,576]{0,1:T(8,128)(2,1)S(1)} %constant_dynamic-slice_fusion), channel_id=1, source_target_pairs={{0,8},{2,10},{4,12},{6,14},{8,0},{9,1},{10,2},{11,3},{12,4},{13,5}... | collective-permute-start | bytes 331784 | tf_op jit(solution)/shard_map/ppermute | solution.py:37
  10.8 8.5 %collective-permute-start = (bf16[96,576]{0,1:T(8,128)(2,1)S(1)}, bf16[96,576]{0,1:T(8,128)(2,1)S(1)}, u32[]{:S(2)}, u32[]{:S(2)}) collective-permute-start(bf16[96,576]{0,1:T(8,128)(2,1)S(1)} %constant_dynamic-slice_fusion), channel_id=1, source_target_pairs={{0,12},{2,14},{4,0},{5,1},{6,2},{7,3},{8,4},{9,5},{10,6},{11,7},{1... | collective-permute-start | bytes 331784 | tf_op jit(solution)/shard_map/ppermute | solution.py:37
  14.1 5.5 %copy-start.2 = (s32[6]{0:T(128)S(1)}, s32[6]{0:T(128)}, u32[]{:S(2)}) copy-start(s32[6]{0:T(128)} %param.9) | copy-start | bytes 76
  19.5 1.9 %collective-permute-start.3 = (bf16[288,576]{0,1:T(8,128)(2,1)S(1)}, bf16[288,576]{0,1:T(8,128)(2,1)S(1)}, u32[]{:S(2)}, u32[]{:S(2)}) collective-permute-start(bf16[288,576]{0,1:T(8,128)(2,1)S(1)} %pad_maximum_fusion), channel_id=1, source_target_pairs={{0,1},{1,0},{2,3},{3,2},{4,5},{5,4},{6,7},{7,6},{8,9},{9,8},{10,11... | collective-permute-start | bytes 995336 | tf_op jit(solution)/shard_map/ppermute | solution.py:41
  34.4 1.8 %collective-permute-start.4 = (bf16[192,1024]{1,0:T(8,128)(2,1)S(1)}, bf16[192,1024]{1,0:T(8,128)(2,1)S(1)}, u32[]{:S(2)}, u32[]{:S(2)}) collective-permute-start(bf16[192,1024]{1,0:T(8,128)(2,1)S(1)} %pad_maximum_fusion.1), channel_id=1, source_target_pairs={{0,1},{1,0},{2,3},{3,2},{4,5},{5,4},{6,7},{7,6},{8,9},{9,8},{10,11... | collective-permute-start | bytes 1179656 | tf_op jit(solution)/shard_map/ppermute | solution.py:106
  37.6 7.2 %collective-permute-start.5 = (bf16[192,512]{1,0:T(8,128)(2,1)S(1)}, bf16[192,512]{1,0:T(8,128)(2,1)S(1)}, u32[]{:S(2)}, u32[]{:S(2)}) collective-permute-start(bf16[192,512]{1,0:T(8,128)(2,1)S(1)} %add_convert_fusion.1), channel_id=1, source_target_pairs={{0,2},{1,3},{2,0},{3,1},{4,6},{5,7},{6,4},{7,5},{8,10},{9,11},{10,... | collective-permute-start | bytes 589832 | tf_op jit(solution)/shard_map/ppermute | solution.py:115
